TPU v7x, 512 devices: a whole 4x4x16 slice. The times are simulated.
512 devices in a mesh: freq: 4 (over y), row: 8 (over x, core), col: 16 (over z).
Axes of the slice: x: 4, y: 4, z: 16, core: 2. Of those that a mesh axis runs over, the one named last changes fastest.
Arguments:
- snapshots: bfloat16 [32, 1024, 128], P('freq', 'col'), may hold values from -60 to 60, as said below
- replicas: bfloat16 [32, 2, 1024, 8192], P('freq', None, 'col', 'row'), may hold values from -64 to 64, as said below
- level_index: int32 [32], P('freq'), may hold values from 0 to 7
- loading_iters: int32 [32], P('freq'), may hold values from 1 to 2
Outputs:
- log_power: float32 [32, 8192], P('freq', ('row', 'col'))
- broadband: float32 [8192], P(('row', 'col'))
Inputs may be any that keep to these rules, and one draw needn't show every extreme that they name: `snapshots`: each frequency's snapshots are independent of the other frequencies' snapshots. `replicas`: each candidate's field is sensor noise plus a part in the span of its frequency's snapshots.
All inputs are finite; a program needn't handle non-finite values.
Results may differ from a plain program's by a relative error of at most 0.0003.
Values may be sent and summed in bfloat16 or wider, within the bound.
A program may use at most 64 MiB of HBM per device.

v0:
```python
import math

import jax
import jax.numpy as jnp
from jax import lax
from jax.sharding import Mesh
from jax.sharding import PartitionSpec as P

M = 1024
LEVELS = 8
ROW_COL = ("row_0", "row_1", "col")
ROW = ("row_0", "row_1")


gain_target = 0.5


def split_up(value, dim, length):
    before, after = (value.shape[:dim], value.shape[dim + 1 :])
    return jnp.moveaxis(value.reshape(*before, length, -1, *after), dim, 0)


def sum_packed(arrays, axis, dims):
    length = lax.axis_size(axis)
    tiles = [split_up(a, dim, length) for a, dim in zip(arrays, dims)]
    lines = jnp.concatenate([b.reshape(length, -1) for b in tiles], axis=1)
    span = max(16, -(-lines.shape[1] // 1024) * 8)
    lines = jnp.pad(lines, ((0, 0), (0, span * 128 - lines.shape[1]))).reshape(-1, 128)
    vector, at, finished = (lax.psum_scatter(lines, axis, tiled=True).reshape(-1), 0, [])
    for b in tiles:
        part = b[0]
        finished.append(vector[at : at + part.size].reshape(part.shape))
        at += part.size
    return tuple(finished)


def filled_up(lines, length):
    spare = -len(lines) % length
    return jnp.pad(lines, [(0, spare)] + [(0, 0)] * (lines.ndim - 1))


def sent_to_all(value, axis):
    copies = jnp.broadcast_to(value, (lax.axis_size(axis), *value.shape))
    return lax.all_to_all(copies, axis, split_axis=0, concat_axis=0, tiled=True)


def joined_along(tiles, dim):
    tiles = jnp.moveaxis(tiles, 0, dim)
    dims = tiles.shape
    return tiles.reshape(*dims[:dim], dims[dim] * dims[dim + 1], *dims[dim + 2 :])


def collect(value, axis, dim):
    tiles = sent_to_all(value, axis)
    return joined_along(tiles, dim)


def sent_and_summed(value, axis, dim):
    tiles = split_up(value, dim, lax.axis_size(axis))
    arrived = lax.all_to_all(tiles, axis, split_axis=0, concat_axis=0, tiled=True)
    return arrived.sum(axis=0)


def sum_by_parts(value, axes):
    lines = value.reshape(-1, value.shape[-1])
    padded = filled_up(lines, lax.axis_size(axes))
    whole = collect(sent_and_summed(padded, axes, 0), axes, 0)
    return lax.slice_in_dim(whole, 0, len(lines)).reshape(value.shape)


def of_everyone(value, axis):
    everything = sent_to_all(value, axis)
    return jnp.sum(everything, axis=0)


def one_axis_at_a_time(value, axes):
    far, near = axes
    return of_everyone(of_everyone(value, near), far)


def stack_snapshots(snaps):
    count = snaps.shape[2] // 2
    real_part = snaps[:, :, :count]
    imag_part = snaps[:, :, count:]
    upper = jnp.concatenate([real_part, -imag_part], 2)
    lower = jnp.concatenate([imag_part, real_part], 2)
    return jnp.concatenate([upper, lower], 1)


def sensor_products(snaps, reps):
    stacked = stack_snapshots(snaps)
    columns = reps.reshape(reps.shape[0], 2 * reps.shape[2], reps.shape[3])
    projected = jnp.einsum("fmk,fmc->fkc", stacked, columns, preferred_element_type=jnp.float32)
    gram_raw = jnp.einsum("fmk,fml->fkl", stacked, stacked, preferred_element_type=jnp.float32)
    wide_cols = columns.astype(jnp.float32)
    norms = jnp.sum(wide_cols * wide_cols, 1)
    return (projected, gram_raw, norms)


def prepare(projected, gram_raw, level_index):
    snap_count = gram_raw.shape[1] // 2
    gram = gram_raw / snap_count
    proj = projected * (1.0 / math.sqrt(snap_count))
    power = jnp.trace(gram, axis1=1, axis2=2) / (2.0 * M)
    steps = jnp.arange(LEVELS)
    levels = 2.0 ** (steps.astype(jnp.float32) / 2.0)
    chosen = jnp.sum(jnp.where(steps[None, :] == level_index[:, None], levels[None, :], 0.0), 1)
    return (gram, proj, power, chosen * power)


def loading_pass(gram, proj, replica_norm, loading):
    dimension = gram.shape[1]
    identity = jnp.eye(dimension, dtype=gram.dtype)
    system = loading[:, None, None] * identity + gram

    def invert(matrix):
        factor = jnp.linalg.cholesky(matrix)
        return jax.scipy.linalg.cho_solve((factor, True), identity)

    inverse = jax.vmap(invert)(system)
    solved = jnp.einsum("fkl,flc->fkc", inverse, proj, precision=lax.Precision.HIGHEST)
    inner_sum = jnp.sum(proj * solved, 1)
    energy = jnp.sum(solved * solved, 1)
    quad_one = (replica_norm - inner_sum) / loading[:, None]
    quad_two = (quad_one - energy) / loading[:, None]
    return (quad_one, quad_two)


def body(snapshots, replicas, level_index, loading_iters):
    col_count = lax.axis_size("col")
    share = replicas.shape[3] // col_count
    projected, gram_raw, replica_norm = sensor_products(snapshots, replicas)
    projected, replica_norm = sum_packed((projected, replica_norm), "col", (2, 1))
    gram_raw = sum_by_parts(gram_raw, "col")
    gram, proj, power, loading_one = prepare(projected, gram_raw, level_index)
    quad_one, quad_two = loading_pass(gram, proj, replica_norm, loading_one)
    gains = quad_one * quad_one / (quad_two * replica_norm)
    gain_total = one_axis_at_a_time(jnp.sum(gains, 1), ("row_0", ("row_1", "col")))
    mean_gain = gain_total / (share * lax.axis_size(ROW) * col_count)
    loading_two = loading_one * (1.0 + (gain_target / mean_gain) ** 2)
    quad_next, unused = loading_pass(gram, proj, replica_norm, loading_two)
    final = jnp.where(loading_iters[:, None] >= 2, quad_next, quad_one)
    log_power = jnp.log(replica_norm / (final * power[:, None]))
    band_total = of_everyone(jnp.sum(log_power, 0), "freq")
    broadband = band_total / (log_power.shape[0] * lax.axis_size("freq"))
    return (log_power, broadband)


def solution(mesh):
    split = Mesh(
        mesh.devices.reshape(mesh.shape["freq"], 4, 2, mesh.shape["col"]),
        ("freq", "row_0", "row_1", "col"),
    )
    return jax.shard_map(
        body,
        mesh=split,
        in_specs=(P("freq", "col", None), P("freq", None, "col", ROW), P("freq"), P("freq")),
        out_specs=(P("freq", ROW_COL), P(ROW_COL)),
        check_vma=False,
    )
```

profile of v0, /device:TPU:1, one launch (start us, length us, event | category | flops | bytes accessed | tf_op | source)
XLA Modules:
  0.0 496.6 jit_solution(18267679807415522003)
XLA Ops:
  7.2 1.2 fusion.20
  8.4 0.1 copy.98
  8.5 0.1 copy.99
  8.7 1.2 fusion.17
  9.9 15.7 %all-to-all-start = ((f32[16,64,128]{2,1,0:T(8,128)}), f32[16,64,128]{2,1,0:T(8,128)S(1)}, u32[]{:S(2)}, u32[]{:S(2)}) async-start(f32[16,64,128]{2,1,0:T(8,128)} %bitcast.5), calls=%async_computation | async-start | bytes 1048576 | tf_op jit(solution)/shard_map/all_to_all | solution.py:60
  25.7 0.0 all-reduce.4.cloned.1.call-start
  25.7 0.5 multiply_reduce_fusion
  26.2 0.1 reshape.121
  26.3 0.1 reshape.122
  26.4 2.9 fusion.18
  29.3 6.9 %copy.72 = f32[16,8,128,64]{3,2,1,0:T(8,128)} copy(f32[16,8,128,64]{2,3,0,1:T(8,128)} %bitcast.42) | data formatting | bytes 8388608 | tf_op jit(solution)/shard_map/transpose | solution.py:20
  36.2 6.0 %reshape.120 = f32[16,65536]{1,0:T(8,128)} reshape(f32[16,8,128,64]{3,2,1,0:T(8,128)} %copy.72) | data formatting | bytes 8388608 | tf_op jit(solution)/shard_map/reshape | solution.py:26
  42.2 4.5 select_maximum_fusion
  46.7 3.9 reshape.123
  50.6 0.0 all-reduce.4.cloned.1.call-update
  50.7 0.9 broadcast_in_dim.67
  51.6 11.5 %all-to-all-start.1 = ((f32[16,64,128]{2,1,0:T(8,128)}), f32[16,64,128]{2,1,0:T(8,128)S(1)}, u32[]{:S(2)}, u32[]{:S(2)}) async-start(f32[16,64,128]{2,1,0:T(8,128)} %broadcast_in_dim.67), calls=%async_computation.1 | async-start | bytes 1048576 | tf_op jit(solution)/shard_map/all_to_all | solution.py:44
  63.1 0.1 copy.74
  63.2 0.1 copy.78
  63.3 1.3 dynamic-slice
  65.3 0.2 select_reduce_fusion.3
  65.5 22.3 %all-to-all-done.1 = f32[16,64,128]{2,1,0:T(8,128)S(1)} async-done(((f32[16,64,128]{2,1,0:T(8,128)}), f32[16,64,128]{2,1,0:T(8,128)S(1)}, u32[]{:S(2)}, u32[]{:S(2)}) %all-to-all-start.1) | async-done | bytes 524320 | tf_op jit(solution)/shard_map/all_to_all | solution.py:44
  87.8 0.2 broadcast_multiply_fusion
  88.0 0.1 reduce_sum.120
  88.1 0.1 reduce_sum.121
  88.2 0.2 copy.76
  88.4 0.1 multiply_add_fusion.1
  88.5 0.2 copy.77
  88.7 0.1 fusion.10
  88.9 0.0 copy-start.2
  88.9 93.8 %custom-call.10 = f32[8,128,128]{2,1,0:T(8,128)S(1)} custom-call(f32[8,128,128]{2,1,0:T(8,128)S(1)} %fusion.10), custom_call_target="Cholesky" | custom-call | tf_op jit(solution)/shard_map/vmap(jit(cholesky))/cholesky | solution.py:117
  182.7 0.1 select_reduce_fusion.1
  182.8 0.1 compare_reduce_fusion.1
  182.9 0.1 select_bitcast_fusion.1
  183.0 78.6 %custom-call.11 = f32[8,1,128,128]{2,3,1,0:T(8,128)S(1)} custom-call(f32[8,1,128,128]{3,2,1,0:T(8,128)S(1)} %select_bitcast_fusion.1), custom_call_target="InvertDiagBlocksLowerTriangular" | custom-call | tf_op jit(solution)/shard_map/vmap(jit(_cho_solve))/triangular_solve | solution.py:118
  261.6 1.0 fusion.8
  262.6 0.7 fusion.6
  263.3 0.0 all-reduce.4.cloned.1.call-done
  263.3 0.7 constant_dynamic-slice_fusion
  264.0 0.1 reshape.124
  264.1 1.0 dynamic-slice_multiply_fusion
  265.1 0.1 mul.93
  265.2 0.2 copy.89
  265.4 1.2 multiply_reduce_fusion.2
  266.6 0.2 divide_reduce_fusion
  266.8 28.8 %all_to_all.28 = f32[32,1,8]{2,1,0:T(1,128)S(1)} all-to-all(f32[32,1,8]{2,1,0:T(1,128)S(1)} %broadcast_in_dim.69), channel_id=1, replica_groups=mesh['freq'=4,'row_0'=4,'row_1'=2,'col'=16] {'row_1','col'}, dimensions={0} | all-to-all | bytes 2048 | tf_op jit(solution)/shard_map/all_to_all | solution.py:44
  295.6 0.1 reduce_sum.125
  295.7 0.6 broadcast_in_dim.70
  296.3 4.0 all-to-all-start.3
  300.3 4.0 all-to-all-done.3
  304.4 0.1 multiply_add_fusion
  304.5 0.2 copy.85
  304.7 0.1 fusion.5
  304.9 93.8 %custom-call.12 = f32[8,128,128]{2,1,0:T(8,128)S(1)} custom-call(f32[8,128,128]{2,1,0:T(8,128)S(1)} %fusion.5), custom_call_target="Cholesky" | custom-call | tf_op jit(solution)/shard_map/vmap(jit(cholesky))/cholesky | solution.py:117
  398.7 0.1 select_reduce_fusion
  398.7 0.1 compare_reduce_fusion
  398.8 0.1 select_bitcast_fusion
  399.0 78.6 %custom-call.13 = f32[8,1,128,128]{2,3,1,0:T(8,128)S(1)} custom-call(f32[8,1,128,128]{3,2,1,0:T(8,128)S(1)} %select_bitcast_fusion), custom_call_target="InvertDiagBlocksLowerTriangular" | custom-call | tf_op jit(solution)/shard_map/vmap(jit(_cho_solve))/triangular_solve | solution.py:118
  477.6 1.0 fusion.3
  478.6 0.7 fusion.1
  479.2 1.2 fusion
  480.4 0.7 fusion.19
  481.1 8.1 %all_to_all.29 = f32[4,1,64]{2,1,0:T(1,128)S(1)} all-to-all(f32[4,1,64]{2,1,0:T(1,128)S(1)} %broadcast_in_dim.71), channel_id=1, replica_groups=mesh['freq'=4,'row_0'=4,'row_1'=2,'col'=16] {'freq'}, dimensions={0} | all-to-all | bytes 2048 | tf_op jit(solution)/shard_map/all_to_all | solution.py:44
  489.2 0.5 broadcast_multiply_fusion.1
  (22 shorter events, 0.3 us)
Async XLA Ops:
  7.2 18.5 %copy-start = (bf16[8,2,64,1024]{3,2,1,0:T(8,128)(2,1)S(1)}, bf16[8,2,64,1024]{3,2,1,0:T(8,128)(2,1)}, u32[]{:S(2)}) copy-start(bf16[8,2,64,1024]{3,2,1,0:T(8,128)(2,1)} %param.8) | copy-start | bytes 6291460
  9.9 40.7 %all-to-all-start = ((f32[16,64,128]{2,1,0:T(8,128)}), f32[16,64,128]{2,1,0:T(8,128)S(1)}, u32[]{:S(2)}, u32[]{:S(2)}) async-start(f32[16,64,128]{2,1,0:T(8,128)} %bitcast.5), calls=%async_computation | async-start | bytes 1048576 | tf_op jit(solution)/shard_map/all_to_all | solution.py:60
  25.7 237.7 %all-reduce.4.cloned.1.call-start = ((), (), s32[]{:S(2)}) async-start(), calls=%async_computation.5 | async-start | bytes 8519680
  50.6 14.7 %copy-start.1 = (s32[8]{0:T(128)S(1)}, s32[8]{0:T(128)}, u32[]{:S(2)}) copy-start(s32[8]{0:T(128)} %param.9) | copy-start | bytes 100
  51.6 36.2 %all-to-all-start.1 = ((f32[16,64,128]{2,1,0:T(8,128)}), f32[16,64,128]{2,1,0:T(8,128)S(1)}, u32[]{:S(2)}, u32[]{:S(2)}) async-start(f32[16,64,128]{2,1,0:T(8,128)} %broadcast_in_dim.67), calls=%async_computation.1 | async-start | bytes 1048576 | tf_op jit(solution)/shard_map/all_to_all | solution.py:44
  88.9 211.4 %copy-start.2 = (s32[8]{0:T(128)S(1)}, s32[8]{0:T(128)}, u32[]{:S(2)}) copy-start(s32[8]{0:T(128)} %param.10) | copy-start | bytes 100
  296.3 8.1 %all-to-all-start.3 = ((f32[4,1,8]{2,1,0:T(1,128)}), f32[4,1,8]{2,1,0:T(1,128)S(1)}, u32[]{:S(2)}, u32[]{:S(2)}) async-start(f32[4,1,8]{2,1,0:T(1,128)} %broadcast_in_dim.70), calls=%async_computation.3 | async-start | bytes 4096 | tf_op jit(solution)/shard_map/all_to_all | solution.py:44
Sparse Core Ops, SparseCore 0:
  50.7 167.8 all-reduce.3
where the time goes:
time: 498 us; the launch traced here: 497 us
  other arithmetic  354 us (71%)
  blocking collectives  36.9 us (7%)
  starting transfers between devices  31.3 us (6%)
  waiting for transfers between devices  26.4 us (5%)
  local copies, waits for them, and re-layouts  23.3 us (5%)
  between operations  15 us (3%)
  matrix products  9.85 us (2%)
    another operation x7, other arithmetic, invert(): factor = jnp.linalg.cholesky(matrix)  188 us
    another operation x5, other arithmetic, invert(): return jax.scipy.linalg.cho_solve((factor, True), identity)  157 us
    all_to_all x2, blocking collectives, sent_to_all(): return lax.all_to_all(copies, axis, split_axis=0, concat_axis=0, tiled=True)  36.9 us
    all_to_all x2, waiting for transfers between devices, sent_to_all(): return lax.all_to_all(copies, axis, split_axis=0, concat_axis=0, tiled=True)  26.3 us
    all_to_all x1, starting transfers between devices, sent_and_summed(): lax.all_to_all(tiles, axis, split_axis=0, concat_axis=0, tiled=True)  15.7 us
    all_to_all x2, starting transfers between devices, sent_to_all(): return lax.all_to_all(copies, axis, split_axis=0, concat_axis=0, tiled=True)  15.5 us
  transfers between devices with their start and end apart: 4, of which 2 were waited for; matrix products, arithmetic and copies ran while one was open for 41% of the time, Pallas kernels for 0%

commit v1 on v0

v1 whole, which is shorter than its diff:
```python
import functools

import jax
import jax.numpy as jnp
from jax import lax
from jax.experimental import pallas as pl
from jax.experimental.pallas import tpu as pltpu
from jax.sharding import PartitionSpec as P

SENSORS = 1024
SNAPS = 64
LEVELS = 8
LANES = 128
HALF = 64
GAIN_TARGET = 0.5
MESH_ID = pl.DeviceIdType.MESH
F32 = jnp.float32


def kernel(
    nf, nr, nz,
    lvl_ref, it_ref, snaps_ref, reps_ref,
    logp_ref, band_ref,
    part, recv, gp, grecv, gall, gram, gain_z, gain_r, band_b,
    rs_s, rs_r, ga_s, ga_r, gb_s, gb_r, gc_s, gc_r, qz_s, qz_r, qr_s, qr_r, fb_s, fb_r,
    *mats,
):
    freqs = nr
    pairs = freqs // 2
    hops = nz // 2
    piece = HALF // nz
    me_f, me_r, me_z = lax.axis_index("freq"), lax.axis_index("row"), lax.axis_index("col")
    lane = lax.broadcasted_iota(jnp.int32, (1, LANES), 1)
    low = lane < HALF
    sign_hi = jnp.where(low, 1.0, -1.0).astype(F32)
    sign_lo = jnp.where(low, -1.0, 1.0).astype(F32)
    rows64 = lax.broadcasted_iota(jnp.int32, (HALF, LANES), 0)
    lanes64 = lax.broadcasted_iota(jnp.int32, (HALF, LANES), 1)
    eye = rows64 == lanes64

    def ahead(me, step, count):
        return lax.rem(me + (step + count), count)

    def remote(src, dst, send, got, axis, peer):
        return pltpu.make_async_remote_copy(
            src_ref=src, dst_ref=dst, send_sem=send, recv_sem=got,
            device_id={axis: peer}, device_id_type=MESH_ID,
        )

    barrier = pltpu.get_barrier_semaphore()
    for axis, me, count in (("col", me_z, nz), ("row", me_r, nr), ("freq", me_f, nf)):
        for o in range(1, count):
            pl.semaphore_signal(barrier, inc=1, device_id={axis: ahead(me, o, count)}, device_id_type=MESH_ID)

    x = snaps_ref[me_r]
    w = lax.dot_general(x, x, (((0,), (0,)), ((), ())), preferred_element_type=F32)
    w_up, w_down = w[:HALF, :], w[HALF:, :]
    turned = pltpu.roll(w_down, HALF, 1)
    compact = w_up + turned * sign_hi
    for j in range(nz):
        gp[j] = compact[j * piece:(j + 1) * piece, :]

    for s in range(pairs):
        prods, norms = [], []
        for f in (2 * s, 2 * s + 1):
            snap = snaps_ref[f].astype(F32)
            stacked = jnp.concatenate([snap * sign_hi, pltpu.roll(snap, HALF, 1)], axis=0)
            cols = reps_ref[f]
            prods.append(jnp.dot(stacked.T.astype(jnp.bfloat16), cols, preferred_element_type=F32))
            wide = cols.astype(F32)
            norms.append(jnp.sum(wide * wide, axis=0, keepdims=True))
        for m in range(nz // 2):
            at = slice(m * LANES, (m + 1) * LANES)
            for pair, top, count in ((prods, s * LANES, LANES), (norms, pairs * LANES + s, 1)):
                a, b = pair[0][:, at], pair[1][:, at]
                part[2 * m, top:top + count, :] = jnp.where(low, a, pltpu.roll(b, HALF, 1))
                part[2 * m + 1, top:top + count, :] = jnp.where(low, pltpu.roll(a, HALF, 1), b)
    for d in range(nz):
        part[d, pairs * LANES + pairs:, :] = jnp.zeros((8 - pairs, LANES), F32)

    pl.semaphore_wait(barrier, (nz - 1) + (nr - 1) + (nf - 1))
    pending = []

    ga = []
    for o in range(1, nz):
        to = ahead(me_z, o, nz)
        c = remote(gp.at[to], grecv.at[me_z], ga_s.at[o], ga_r.at[o], "col", to)
        c.start()
        ga.append(c)

    def gram_second():
        total = gp[me_z]
        for o in range(1, nz):
            ga[o - 1].wait_recv()
        for o in range(1, nz):
            total = total + grecv[ahead(me_z, -o, nz)]
        pending.extend(ga)
        gall[me_r, me_z] = total
        for o in range(1, nz):
            c = remote(gall.at[me_r, me_z], gall.at[me_r, me_z], gb_s.at[o], gb_r.at[o], "col", ahead(me_z, o, nz))
            c.start()
            gb.append(c)

    gb, gc = [], []

    def gram_third():
        for c in gb:
            c.wait_recv()
        pending.extend(gb)
        for o in range(1, nr):
            c = remote(gall.at[me_r], gall.at[me_r], gc_s.at[o], gc_r.at[o], "row", ahead(me_r, o, nr))
            c.start()
            gc.append(c)

    powers, loads_one = [], []

    def set_system(f, load):
        mats[f][...] = gram[f] + jnp.where(eye, load, 0.0)

    def gram_done():
        for c in gc:
            c.wait_recv()
        pending.extend(gc)
        for f in range(freqs):
            for j in range(nz):
                gram[f, j * piece:(j + 1) * piece, :] = gall[f, j] * (1.0 / SNAPS)
        for f in range(freqs):
            diag = jnp.sum(jnp.where(eye, gram[f], 0.0), axis=0, keepdims=True)
            power = 2.0 * jnp.sum(diag, axis=1, keepdims=True) / (2.0 * SENSORS)
            level = lvl_ref[f]
            chosen = jnp.float32(0.0)
            for n in range(LEVELS):
                chosen = jnp.where(level == n, jnp.float32(2.0 ** (n / 2.0)), chosen)
            powers.append(power)
            loads_one.append(chosen * power)
            set_system(f, loads_one[f])

    def sweep(first, last):
        def one(k, carry):
            at_re = lane == k
            at_im = lane == k + HALF
            either = at_re | at_im
            ups, turns, res, ims, tiles = [], [], [], [], []
            for f in range(freqs):
                row = mats[f][pl.ds(k, 1), :]
                tile = mats[f][...]
                res.append(jnp.sum(jnp.where(at_re, tile, 0.0), axis=1, keepdims=True))
                ims.append(jnp.sum(jnp.where(at_im, tile, 0.0), axis=1, keepdims=True))
                pivot = jnp.sum(jnp.where(at_re, row, 0.0), axis=1, keepdims=True)
                up = jnp.where(at_re, -1.0, jnp.where(at_im, 0.0, row))
                turn = pltpu.roll(up, HALF, 1) * sign_lo
                inv = 1.0 / pivot
                ups.append(up * inv)
                turns.append(turn * inv)
            for f in range(freqs):
                tile = jnp.where(either, 0.0, mats[f][...])
                mats[f][...] = tile - res[f] * ups[f] - ims[f] * turns[f]
                mats[f][pl.ds(k, 1), :] = ups[f]
            return carry

        lax.fori_loop(first, last, one, 0)

    def arm(s, way):
        return hops if (s < (pairs + 1) // 2) == (way == 0) else hops - 1

    def span(s):
        return slice(s * LANES, (s + 1) * LANES + (8 if s == pairs - 1 else 0))

    rs = {}

    def send(way, t, s):
        sign = 1 if way == 0 else -1
        sp = span(s)
        rows = pl.ds(sp.start, sp.stop - sp.start)
        dest = ahead(me_z, sign * (arm(s, way) - t), nz)
        if t == 0:
            src = part.at[dest, rows]
        else:
            rs[way, t - 1, s].wait_recv()
            recv[way, t - 1, sp, :] = recv[way, t - 1, sp, :] + part[dest, sp, :]
            src = recv.at[way, t - 1, rows]
        c = remote(src, recv.at[way, t, rows], rs_s.at[way, t, s], rs_r.at[way, t, s], "col", ahead(me_z, sign, nz))
        c.start()
        rs[way, t, s] = c
        pending.append(c)

    total_steps = hops * pairs
    second = min(max(1, total_steps // 8), total_steps - 1)
    third = min(max(2, total_steps * 5 // 16), total_steps - 1)
    done = max(third, total_steps // 2 - 1)
    sweeps = list(range(done + 1, total_steps - 1))
    cuts = [HALF * i // len(sweeps) for i in range(len(sweeps) + 1)] if sweeps else []
    step = 0
    for t in range(hops):
        for s in range(pairs):
            for way in (0, 1):
                if t < arm(s, way):
                    send(way, t, s)
            if step == second:
                gram_second()
            if step == third:
                gram_third()
            if step == done:
                gram_done()
            if step in sweeps:
                i = sweeps.index(step)
                sweep(cuts[i], cuts[i + 1])
            step += 1
    if not sweeps:
        sweep(0, HALF)

    proj, norm = [], []
    for s in range(pairs):
        sp = span(s)
        total = part[me_z, sp, :]
        for way in (0, 1):
            last = arm(s, way) - 1
            rs[way, last, s].wait_recv()
            total = total + recv[way, last, sp, :]
        proj.append(total[:LANES] * (1.0 / 8.0))
    extra = total[LANES:]
    for s in range(pairs):
        norm.append(extra[s:s + 1, :])

    def by_half(values, s):
        return jnp.where(low, values[2 * s], values[2 * s + 1])

    def solve(s):
        got = []
        for f in (2 * s, 2 * s + 1):
            inverse = -mats[f][...]
            full = jnp.concatenate([inverse * sign_hi, pltpu.roll(inverse, HALF, 1)], axis=0)
            got.append(jnp.dot(full, proj[s], precision=lax.Precision.HIGHEST, preferred_element_type=F32))
        z = jnp.where(low, got[0], got[1])
        return (
            jnp.sum(proj[s] * z, axis=0, keepdims=True),
            jnp.sum(z * z, axis=0, keepdims=True),
        )

    ones = []
    mine = jnp.zeros((1, LANES), F32)
    for s in range(pairs):
        inner, energy = solve(s)
        load = by_half(loads_one, s)
        quad_one = (norm[s] - inner) / load
        quad_two = (quad_one - energy) / load
        gains = quad_one * quad_one / (quad_two * norm[s])
        left = jnp.sum(jnp.where(low, gains, 0.0), axis=1, keepdims=True)
        right = jnp.sum(jnp.where(low, 0.0, gains), axis=1, keepdims=True)
        mine = mine + jnp.where(lane == 2 * s, left, 0.0) + jnp.where(lane == 2 * s + 1, right, 0.0)
        ones.append(quad_one)

    def everyone(buf, me, count, axis, send_sem, recv_sem, value):
        buf[me] = value
        copies = []
        for o in range(1, count):
            c = remote(buf.at[me], buf.at[me], send_sem.at[o], recv_sem.at[o], axis, ahead(me, o, count))
            c.start()
            copies.append(c)
        for c in copies:
            c.wait_recv()
        pending.extend(copies)
        total = buf[0]
        for i in range(1, count):
            total = total + buf[i]
        return total

    whole = everyone(gain_z, me_z, nz, "col", qz_s, qz_r, mine)
    whole = everyone(gain_r, me_r, nr, "row", qr_s, qr_r, whole)
    mean_gain = whole / (HALF * nz * nr)
    for f in range(freqs):
        mean = jnp.sum(jnp.where(lane == f, mean_gain, 0.0), axis=1, keepdims=True)
        ratio = GAIN_TARGET / mean
        set_system(f, loads_one[f] * (1.0 + ratio * ratio))
    loads_two = []
    for f in range(freqs):
        mean = jnp.sum(jnp.where(lane == f, mean_gain, 0.0), axis=1, keepdims=True)
        ratio = GAIN_TARGET / mean
        loads_two.append(loads_one[f] * (1.0 + ratio * ratio))
    sweep(0, HALF)

    band = jnp.zeros((1, LANES), F32)
    for s in range(pairs):
        inner, _ = solve(s)
        quad_next = (norm[s] - inner) / by_half(loads_two, s)
        iters = jnp.where(low, it_ref[2 * s], it_ref[2 * s + 1])
        final = jnp.where(iters >= 2, quad_next, ones[s])
        log_power = jnp.log(norm[s] / (final * by_half(powers, s)))
        other = pltpu.roll(log_power, HALF, 1)
        logp_ref[2 * s:2 * s + 1, :] = log_power[:, :HALF]
        logp_ref[2 * s + 1:2 * s + 2, :] = other[:, :HALF]
        band = band + log_power + other
    band = everyone(band_b, me_f, nf, "freq", fb_s, fb_r, band)
    band_ref[...] = band[:, :HALF] / (freqs * nf)

    for c in pending:
        c.wait_send()


def solution(mesh):
    nf, nr, nz = mesh.shape["freq"], mesh.shape["row"], mesh.shape["col"]
    pairs, hops = nr // 2, nz // 2
    rows = pairs * LANES + 8
    dma = pltpu.SemaphoreType.DMA

    def body(snapshots, replicas, level_index, loading_iters):
        freqs, sensors, cands = snapshots.shape[0], snapshots.shape[1], replicas.shape[3]
        vmem = pl.BlockSpec(memory_space=pltpu.VMEM)
        smem = pl.BlockSpec(memory_space=pltpu.SMEM)
        log_power, band = pl.pallas_call(
            functools.partial(kernel, nf, nr, nz),
            out_shape=(
                jax.ShapeDtypeStruct((freqs, HALF), F32),
                jax.ShapeDtypeStruct((1, HALF), F32),
            ),
            in_specs=[smem, smem, vmem, vmem],
            out_specs=(vmem, vmem),
            scratch_shapes=[
                pltpu.VMEM((nz, rows, LANES), F32),
                pltpu.VMEM((2, hops, rows, LANES), F32),
                pltpu.VMEM((nz, HALF // nz, LANES), F32),
                pltpu.VMEM((nz, HALF // nz, LANES), F32),
                pltpu.VMEM((nr, nz, HALF // nz, LANES), F32),
                pltpu.VMEM((nr, HALF, LANES), F32),
                pltpu.VMEM((nz, 1, LANES), F32),
                pltpu.VMEM((nr, 1, LANES), F32),
                pltpu.VMEM((nf, 1, LANES), F32),
                dma((2, hops, pairs)), dma((2, hops, pairs)),
                dma((nz,)), dma((nz,)),
                dma((nz,)), dma((nz,)),
                dma((nr,)), dma((nr,)),
                dma((nz,)), dma((nz,)),
                dma((nr,)), dma((nr,)),
                dma((nf,)), dma((nf,)),
                *[pltpu.VMEM((HALF, LANES), F32)] * nr,
            ],
            compiler_params=pltpu.CompilerParams(collective_id=0, has_side_effects=True),
            name="mvdr",
        )(level_index, loading_iters, snapshots, replicas.reshape(freqs, 2 * sensors, cands))
        return log_power, band.reshape(HALF)

    return jax.shard_map(
        body,
        mesh=mesh,
        in_specs=(P("freq", "col", None), P("freq", None, "col", "row"), P("freq"), P("freq")),
        out_specs=(P("freq", ("row", "col")), P(("row", "col"))),
        check_vma=False,
    )
```

time: 498 us -> 108 us (0.22)
  other arithmetic: 354 us -> 0 us
  Pallas kernels: 0 us -> 105 us
  blocking collectives: 36.9 us -> 0 us
  starting transfers between devices: 31.3 us -> 0 us
  waiting for transfers between devices: 26.4 us -> 0 us
  local copies, waits for them, and re-layouts: 23.3 us -> 2.4 us
  between operations: 15 us -> 0.64 us
  matrix products: 9.85 us -> 0 us
    another operation x12 -> x0, other arithmetic: 345 us -> none  [the longest x7 188 us: invert(): factor = jnp.linalg.cholesky(matrix)]
    pallas_call x0 -> x1, Pallas kernels: none -> 105 us  [body(): pl.pallas_call(functools.partial(kernel, nf, nr, nz), out_shape=(jax.Shap...]
    all_to_all x2 -> x0, blocking collectives: 36.9 us -> none  [sent_to_all(): return lax.all_to_all(copies, axis, split_axis=0, concat_axis=0, tiled=True)]
    all_to_all x3 -> x0, starting transfers between devices: 31.2 us -> none  [the longest x1 15.7 us: sent_and_summed(): lax.all_to_all(tiles, axis, split_axis=0, concat_axis=0, tiled=True)]
    all_to_all x3 -> x0, waiting for transfers between devices: 26.3 us -> none  [the longest x2 26.3 us: sent_to_all(): return lax.all_to_all(copies, axis, split_axis=0, concat_axis=0, tiled=True)]
    reshape x5 -> x0, local copies, waits for them, and re-layouts: 10.1 us -> none  [the longest x2 6.09 us: sum_packed(): lines = jnp.concatenate([b.reshape(length, -1) for b in tiles], axis=1)]
    transpose x2 -> x0, local copies, waits for them, and re-layouts: 6.94 us -> none  [split_up(): return jnp.moveaxis(value.reshape(*before, length, -1, *after), dim, 0)]
    dot_general x4 -> x0, matrix products: 6.52 us -> none  [the longest x1 2.94 us: sensor_products(): jnp.einsum('fmk,fmc->fkc', stacked, columns, preferred_element_type=jnp.f...]
  transfers between devices with their start and end apart: 4 -> 0, of which waited for: 2 -> 0; matrix products, arithmetic and copies ran while one was open for 41% -> 0% of each run, Pallas kernels for 0% -> 0%
where the time goes in v1:
time: 108 us
  Pallas kernels  105 us (97%)
  local copies, waits for them, and re-layouts  2.4 us (2%)
    pallas_call x1, Pallas kernels, body(): pl.pallas_call(functools.partial(kernel, nf, nr, nz), out_shape=(jax.Shap...  105 us
    unnamed x2, local copies, waits for them, and re-layouts  2.4 us

profile of v1, /device:TPU:1, one launch (start us, length us, event | category | flops | bytes accessed | tf_op | source)
XLA Modules:
  0.0 108.0 jit_solution(6988320887699516438)
XLA Ops:
  0.6 105.0 %mvdr.1 = (f32[8,64]{1,0:T(8,128)}, f32[1,64]{1,0:T(1,128)}) custom-call(s32[8]{0:T(128)} %lvl_ref.1, s32[8]{0:T(128)} %it_ref.1, bf16[8,64,128]{2,1,0:T(8,128)(2,1)} %snaps_ref.1, bf16[8,128,1024]{2,1,0:T(8,128)(2,1)} %bitcast.2), custom_call_target="tpu_custom_call" | custom-call | tf_op jit(solution)/shard_map/mvdr/pallas_call | solution.py:310
  105.6 1.3 %copy.8 = f32[8,64]{1,0:T(8,128)} copy(f32[8,64]{1,0:T(8,128)} %get-tuple-element.8) | data formatting | bytes 4096
  106.9 1.1 %copy.9 = f32[64]{0:T(128)} copy(f32[64]{0:T(128)} %bitcast.3) | data formatting | bytes 512

commit v2 on v1

v2 whole, which is shorter than its diff:
```python
import functools

import jax
import jax.numpy as jnp
from jax import lax
from jax.experimental import pallas as pl
from jax.experimental.pallas import tpu as pltpu
from jax.sharding import PartitionSpec as P

SENSORS = 1024
SNAPS = 64
LEVELS = 8
LANES = 128
HALF = 64
EXTRA = 8
GAIN_TARGET = 0.5
MESH_ID = pl.DeviceIdType.MESH
F32 = jnp.float32


def kernel(
    nf, nr, nz,
    lvl_ref, it_ref, snaps_ref, reps_hbm,
    out_ref,
    reps, part, recv, gather, mat, gram, xsend, xrecv, gain, lsend, lrecv,
    in_sem, rs_s, rs_r, ga_s, ga_r, xx_s, xx_r, qz_s, qz_r, ll_s, ll_r,
):
    freqs = nr
    pairs = freqs // 2
    blocks = nr // 2
    hops = nz // 2
    me_f, me_r, me_z = lax.axis_index("freq"), lax.axis_index("row"), lax.axis_index("col")
    lane = lax.broadcasted_iota(jnp.int32, (1, LANES), 1)
    low = lane < HALF
    sign_hi = jnp.where(low, 1.0, -1.0).astype(F32)
    sign_lo = jnp.where(low, -1.0, 1.0).astype(F32)
    eye = lax.broadcasted_iota(jnp.int32, (HALF, LANES), 0) == lax.broadcasted_iota(jnp.int32, (HALF, LANES), 1)

    def swap(v):
        return pltpu.roll(v, HALF, 1)

    def ahead(me, step, count):
        return lax.rem(me + (step + count), count)

    def remote(src, dst, send, got, peer):
        return pltpu.make_async_remote_copy(
            src_ref=src, dst_ref=dst, send_sem=send, recv_sem=got, device_id=peer, device_id_type=MESH_ID,
        )

    barrier = pltpu.get_barrier_semaphore()
    greet = [("col", ahead(me_z, 1, nz)), ("col", ahead(me_z, -1, nz))]
    greet += [("row", ahead(me_r, o, nr)) for o in range(1, nr)]
    greet += [("freq", ahead(me_f, o, nf)) for o in range(1, nf)]
    for axis, peer in greet:
        pl.semaphore_signal(barrier, inc=1, device_id={axis: peer}, device_id_type=MESH_ID)

    fetch = []
    for s in range(pairs):
        c = pltpu.make_async_copy(reps_hbm.at[pl.ds(2 * s, 2)], reps.at[pl.ds(2 * s, 2)], in_sem.at[s])
        c.start()
        fetch.append(c)

    for s in range(pairs):
        fetch[s].wait()
        prods, norms = [], []
        for f in (2 * s, 2 * s + 1):
            snap = snaps_ref[f].astype(F32)
            stacked = jnp.concatenate([snap * sign_hi, swap(snap)], axis=0)
            cols = reps[f]
            prods.append(jnp.dot(stacked.T.astype(jnp.bfloat16), cols, preferred_element_type=F32))
            wide = cols.astype(F32)
            norms.append(jnp.sum(wide * wide, axis=0, keepdims=True))
        for m in range(nz // 2):
            at = slice(m * LANES, (m + 1) * LANES)
            for pair, top, count in ((prods, s * LANES, LANES), (norms, pairs * LANES + s, 1)):
                a, b = pair[0][:, at], pair[1][:, at]
                part[2 * m, top:top + count, :] = jnp.where(low, a, swap(b))
                part[2 * m + 1, top:top + count, :] = jnp.where(low, swap(a), b)
    for d in range(nz):
        part[d, pairs * LANES + pairs:, :] = jnp.zeros((EXTRA - pairs, LANES), F32)
    gather[me_z] = snaps_ref[me_r]

    pl.semaphore_wait(barrier, len(greet))
    pending = []

    ring = {}

    def pass_on(h):
        for way, sign, reach in ((0, 1, hops), (1, -1, hops - 1)):
            if h < reach:
                slot = ahead(me_z, -sign * h, nz)
                if h == 0:
                    src = snaps_ref.at[me_r]
                else:
                    ring[way, h - 1].wait_recv()
                    src = gather.at[slot]
                c = remote(src, gather.at[slot], ga_s.at[way, h], ga_r.at[way, h], {"col": ahead(me_z, sign, nz)})
                c.start()
                ring[way, h] = c
                pending.append(c)

    found = {}

    def gram_done():
        ring[0, hops - 1].wait_recv()
        if hops > 1:
            ring[1, hops - 2].wait_recv()
        x = gather[...].reshape(nz * HALF, LANES)
        w = lax.dot_general(x, x, (((0,), (0,)), ((), ())), preferred_element_type=F32)
        gram[...] = (w[:HALF, :] + swap(w[HALF:, :]) * sign_hi) * (1.0 / SNAPS)
        diag = jnp.sum(jnp.where(eye, gram[...], 0.0), axis=0, keepdims=True)
        power = 2.0 * jnp.sum(diag, axis=1, keepdims=True) / (2.0 * SENSORS)
        level = lvl_ref[me_r]
        chosen = jnp.float32(0.0)
        for n in range(LEVELS):
            chosen = jnp.where(level == n, jnp.float32(2.0 ** (n / 2.0)), chosen)
        found["power"] = power
        found["load"] = chosen * power
        set_system(found["load"])

    def set_system(load):
        mat[...] = gram[...] + jnp.where(eye, load, 0.0)

    def sweep(first, last):
        def at(v, where):
            return jnp.sum(jnp.where(where, v, 0.0), axis=1, keepdims=True)

        def one(i, carry):
            k = 2 * i
            re0, re1 = lane == k, lane == k + 1
            im0, im1 = lane == k + HALF, lane == k + (HALF + 1)
            pivots = re0 | re1 | im0 | im1
            tile = mat[...]
            row0, row1 = mat[pl.ds(k, 1), :], mat[pl.ds(k + 1, 1), :]
            c0r, c0i, c1r, c1i = at(tile, re0), at(tile, im0), at(tile, re1), at(tile, im1)
            a, br, bi, c = at(row0, re0), at(row0, re1), at(row0, im1), at(row1, re1)
            r0 = jnp.where(re0, -1.0, jnp.where(pivots, 0.0, row0))
            r1 = jnp.where(re1, -1.0, jnp.where(pivots, 0.0, row1))
            j0, j1 = swap(r0) * sign_lo, swap(r1) * sign_lo
            inv = 1.0 / (a * c - (br * br + bi * bi))
            ca, cc, cr, ci = a * inv, c * inv, br * inv, bi * inv
            u0 = cc * r0 - (cr * r1 + ci * j1)
            u1 = ca * r1 - (cr * r0 - ci * j0)
            w0 = cc * j0 - (cr * j1 - ci * r1)
            w1 = ca * j1 - (cr * j0 + ci * r0)
            tile = jnp.where(pivots, 0.0, tile)
            mat[...] = tile - (c0r * u0 + c0i * w0) - (c1r * u1 + c1i * w1)
            mat[pl.ds(k, 1), :] = u0
            mat[pl.ds(k + 1, 1), :] = u1
            return carry

        lax.fori_loop(first, last, one, 0)

    def arm(s, way):
        return hops if (s < (pairs + 1) // 2) == (way == 0) else hops - 1

    def span(s):
        return slice(s * LANES, (s + 1) * LANES + (EXTRA if s == pairs - 1 else 0))

    rs = {}

    def send(way, t, s):
        sign = 1 if way == 0 else -1
        sp = span(s)
        rows = pl.ds(sp.start, sp.stop - sp.start)
        dest = ahead(me_z, sign * (arm(s, way) - t), nz)
        if t == 0:
            src = part.at[dest, rows]
        else:
            rs[way, t - 1, s].wait_recv()
            recv[way, t - 1, sp, :] = recv[way, t - 1, sp, :] + part[dest, sp, :]
            src = recv.at[way, t - 1, rows]
        c = remote(src, recv.at[way, t, rows], rs_s.at[way, t, s], rs_r.at[way, t, s], {"col": ahead(me_z, sign, nz)})
        c.start()
        rs[way, t, s] = c
        pending.append(c)

    order = [pairs - 1] + list(range(pairs - 1))
    total_steps = hops * pairs
    gap = 2 if total_steps >= 4 * hops else 1
    done = min(gap * hops + 1, total_steps - 1)
    sweeps = list(range(done + 1, total_steps - 1))
    pivots = HALF // 2
    cuts = [pivots * i // len(sweeps) for i in range(len(sweeps) + 1)] if sweeps else []
    step = 0
    pass_on(0)
    next_hop = 1
    for t in range(hops):
        for s in order:
            for way in (0, 1):
                if t < arm(s, way):
                    send(way, t, s)
            if step >= gap * next_hop and next_hop < hops:
                pass_on(next_hop)
                next_hop += 1
            if step == done:
                while next_hop < hops:
                    pass_on(next_hop)
                    next_hop += 1
                gram_done()
            if step in sweeps:
                i = sweeps.index(step)
                sweep(cuts[i], cuts[i + 1])
            step += 1
    if not sweeps:
        sweep(0, pivots)

    outgoing = {}
    norms = None
    for s in order:
        sp = span(s)
        total = part[me_z, sp, :]
        for way in (0, 1):
            last = arm(s, way) - 1
            rs[way, last, s].wait_recv()
            total = total + recv[way, last, sp, :]
        if s == pairs - 1:
            norms = total[LANES:]
        up, down = total[:HALF], total[HALF:LANES]
        norm = norms[s:s + 1, :]
        for f, packed, row in (
            (2 * s, jnp.where(low, up, swap(down)), norm),
            (2 * s + 1, jnp.where(low, swap(up), down), swap(norm)),
        ):
            xsend[f, :HALF, :] = packed
            xsend[f, HALF:, :] = jnp.broadcast_to(row, (EXTRA, LANES))
            c = remote(xsend.at[f], xrecv.at[me_r], xx_s.at[f], xx_r.at[me_r], {"row": f})
            outgoing[f] = c

            @pl.when(me_r != f)
            def _(c=c):
                c.start()

            @pl.when(me_r == f)
            def _(f=f):
                xrecv[f] = xsend[f]

    for q in range(nr):
        @pl.when(me_r != q)
        def _(q=q):
            remote(xsend.at[q], xrecv.at[q], xx_s.at[q], xx_r.at[q], {"row": q}).wait_recv()

    proj, norm = [], []
    for m in range(blocks):
        a, b = xrecv[2 * m], xrecv[2 * m + 1]
        proj.append(jnp.concatenate([
            jnp.where(low, a[:HALF], swap(b[:HALF])),
            jnp.where(low, swap(a[:HALF]), b[:HALF]),
        ], axis=0) * (1.0 / 8.0))
        norm.append(jnp.where(low, a[HALF:HALF + 1], swap(b[HALF:HALF + 1])))
    proj = jnp.concatenate(proj, axis=1)
    norm = jnp.concatenate(norm, axis=1)

    def solve():
        inverse = -mat[...]
        full = jnp.concatenate([inverse * sign_hi, swap(inverse)], axis=0)
        return jnp.dot(full, proj, precision=lax.Precision.HIGHEST, preferred_element_type=F32)

    z = solve()
    inner = jnp.sum(proj * z, axis=0, keepdims=True)
    energy = jnp.sum(z * z, axis=0, keepdims=True)
    load_one = found["load"]
    first_quad = (norm - inner) / load_one
    quad_two = (first_quad - energy) / load_one
    gains = first_quad * first_quad / (quad_two * norm)
    mine = jnp.sum(gains, axis=1, keepdims=True)

    gain[me_z] = jnp.broadcast_to(mine, (1, LANES))
    copies = []
    for o in range(1, nz):
        c = remote(gain.at[me_z], gain.at[me_z], qz_s.at[o], qz_r.at[o], {"col": ahead(me_z, o, nz)})
        c.start()
        copies.append(c)
    for c in copies:
        c.wait_recv()
    pending.extend(copies)
    whole = gain[0]
    for i in range(1, nz):
        whole = whole + gain[i]
    mean_gain = whole / (HALF * nz * nr)
    ratio = GAIN_TARGET / mean_gain[:, :1]
    load_two = load_one * (1.0 + ratio * ratio)
    set_system(load_two)
    sweep(0, pivots)

    z = solve()
    quad_next = (norm - jnp.sum(proj * z, axis=0, keepdims=True)) / load_two
    final = jnp.where(it_ref[me_r] >= 2, quad_next, first_quad)
    log_power = jnp.log(norm / (final * found["power"]))
    for m in range(blocks):
        block = log_power[:, m * LANES:(m + 1) * LANES]
        lsend[2 * m] = block
        lsend[2 * m + 1] = swap(block)

    lrecv[me_f, me_r] = lsend[me_r]
    copies = []
    for of in range(nf):
        for o in range(nr):
            if of or o:
                to_f, to_r = ahead(me_f, of, nf), ahead(me_r, o, nr)
                c = remote(lsend.at[to_r], lrecv.at[me_f, me_r], ll_s.at[of, o], ll_r.at[of, o], {"freq": to_f, "row": to_r})
                c.start()
                copies.append(c)
    for c in copies:
        c.wait_recv()
    pending.extend(copies)
    band = jnp.zeros((1, LANES), F32)
    for f in range(nf):
        for r in range(nr):
            band = band + lrecv[f, r]
    for r in range(nr):
        out_ref[r:r + 1, :] = lrecv[me_f, r]
    out_ref[nr:, :] = jnp.broadcast_to(band / (freqs * nf), (EXTRA, LANES))

    for c in pending:
        c.wait_send()
    for f in range(freqs):
        @pl.when(me_r != f)
        def _(f=f):
            outgoing[f].wait_send()


def split_result(both_ref, logp_ref, band_ref):
    rows = logp_ref.shape[0]
    logp_ref[...] = both_ref[:rows, :HALF]
    band_ref[...] = both_ref[rows:rows + 1, :HALF]


def solution(mesh):
    nf, nr, nz = mesh.shape["freq"], mesh.shape["row"], mesh.shape["col"]
    pairs, hops = nr // 2, nz // 2
    rows = pairs * LANES + EXTRA
    dma = pltpu.SemaphoreType.DMA

    def body(snapshots, replicas, level_index, loading_iters):
        freqs, sensors, cands = snapshots.shape[0], snapshots.shape[1], replicas.shape[3]
        vmem = pl.BlockSpec(memory_space=pltpu.VMEM)
        smem = pl.BlockSpec(memory_space=pltpu.SMEM)
        both = pl.pallas_call(
            functools.partial(kernel, nf, nr, nz),
            out_shape=jax.ShapeDtypeStruct((freqs + EXTRA, LANES), F32),
            in_specs=[smem, smem, vmem, pl.BlockSpec(memory_space=pl.ANY)],
            out_specs=vmem,
            scratch_shapes=[
                pltpu.VMEM((freqs, 2 * sensors, cands), jnp.bfloat16),
                pltpu.VMEM((nz, rows, LANES), F32),
                pltpu.VMEM((2, hops, rows, LANES), F32),
                pltpu.VMEM((nz, sensors, LANES), jnp.bfloat16),
                pltpu.VMEM((HALF, LANES), F32),
                pltpu.VMEM((HALF, LANES), F32),
                pltpu.VMEM((nr, HALF + EXTRA, LANES), F32),
                pltpu.VMEM((nr, HALF + EXTRA, LANES), F32),
                pltpu.VMEM((nz, 1, LANES), F32),
                pltpu.VMEM((nr, 1, LANES), F32),
                pltpu.VMEM((nf, nr, 1, LANES), F32),
                dma((pairs,)),
                dma((2, hops, pairs)), dma((2, hops, pairs)),
                dma((2, hops)), dma((2, hops)),
                dma((nr,)), dma((nr,)),
                dma((nz,)), dma((nz,)),
                dma((nf, nr)), dma((nf, nr)),
            ],
            compiler_params=pltpu.CompilerParams(collective_id=0, has_side_effects=True),
            name="mvdr",
        )(level_index, loading_iters, snapshots, replicas.reshape(freqs, 2 * sensors, cands))
        log_power, band = pl.pallas_call(
            split_result,
            out_shape=(
                jax.ShapeDtypeStruct((freqs, HALF), F32),
                jax.ShapeDtypeStruct((1, HALF), F32),
            ),
            in_specs=[vmem],
            out_specs=(vmem, vmem),
            name="split",
        )(both)
        return log_power, band.reshape(HALF)

    return jax.shard_map(
        body,
        mesh=mesh,
        in_specs=(P("freq", "col", None), P("freq", None, "col", "row"), P("freq"), P("freq")),
        out_specs=(P("freq", ("row", "col")), P(("row", "col"))),
        check_vma=False,
    )
```

time: 108 us -> 91.6 us (0.85)
  Pallas kernels: 105 us -> 90.7 us
  local copies, waits for them, and re-layouts: 2.4 us -> 0 us
    pallas_call x1 -> x2, Pallas kernels: 105 us -> 90.7 us  [the longest x1 89.4 us: body(): pl.pallas_call(functools.partial(kernel, nf, nr, nz), out_shape=jax.Shape...]
    unnamed x2 -> x0, local copies, waits for them, and re-layouts: 2.4 us -> none
where the time goes in v2:
time: 91.6 us; the launch traced here: 91.4 us
  Pallas kernels  90.7 us (99%)
    pallas_call x1, Pallas kernels, body(): pl.pallas_call(functools.partial(kernel, nf, nr, nz), out_shape=jax.Shape...  89.4 us

profile of v2, /device:TPU:1, one launch (start us, length us, event | category | flops | bytes accessed | tf_op | source)
XLA Modules:
  0.0 91.4 jit_solution(5180074923185372909)
XLA Ops:
  0.6 89.4 %mvdr.1.both_ref = f32[16,128]{1,0:T(8,128)} custom-call(s32[8]{0:T(128)} %lvl_ref.1, s32[8]{0:T(128)} %it_ref.1, bf16[8,64,128]{2,1,0:T(8,128)(2,1)} %snaps_ref.1, bf16[8,128,1024]{2,1,0:T(8,128)(2,1)} %bitcast.2), custom_call_target="tpu_custom_call" | custom-call | tf_op jit(solution)/shard_map/mvdr/pallas_call | solution.py:339
  90.1 1.3 %split.1 = (f32[8,64]{1,0:T(8,128)}, f32[1,64]{1,0:T(1,128)}) custom-call(f32[16,128]{1,0:T(8,128)} %mvdr.1.both_ref), custom_call_target="tpu_custom_call" | custom-call | tf_op jit(solution)/shard_map/split/pallas_call | solution.py:366

commit v3 on v2

--- a/solution.py
+++ b/solution.py
@@ -13,6 +13,10 @@
 LANES = 128
 HALF = 64
 EXTRA = 8
+WORDS = 88
+THIRD = 40
+FIELD = 21
+TOP = 1048575.0
 GAIN_TARGET = 0.5
 MESH_ID = pl.DeviceIdType.MESH
 F32 = jnp.float32
@@ -20,10 +24,11 @@
 
 def kernel(
     nf, nr, nz,
-    lvl_ref, it_ref, snaps_ref, reps_hbm,
+    lvl_hbm, it_hbm, snaps_hbm, reps_hbm,
     out_ref,
-    reps, part, recv, gather, mat, gram, xsend, xrecv, gain, lsend, lrecv,
-    in_sem, rs_s, rs_r, ga_s, ga_r, xx_s, xx_r, qz_s, qz_r, ll_s, ll_r,
+    lvl_ref, it_ref, snaps_ref, reps, part, part_n, first_w, first_n, recv_w, recv_n,
+    gather, mat, gram, xsend, xrecv, gain, lsend, lrecv,
+    in_sem, rs_s, rs_r, rn_s, rn_r, ga_s, ga_r, xx_s, xx_r, qz_s, qz_r, ll_s, ll_r,
 ):
     freqs = nr
     pairs = freqs // 2
@@ -54,11 +59,19 @@
     for axis, peer in greet:
         pl.semaphore_signal(barrier, inc=1, device_id={axis: peer}, device_id_type=MESH_ID)
 
+    small = []
+    for i, (src, dst) in enumerate(((snaps_hbm, snaps_ref), (lvl_hbm, lvl_ref), (it_hbm, it_ref))):
+        c = pltpu.make_async_copy(src, dst, in_sem.at[pairs + i])
+        c.start()
+        small.append(c)
     fetch = []
     for s in range(pairs):
         c = pltpu.make_async_copy(reps_hbm.at[pl.ds(2 * s, 2)], reps.at[pl.ds(2 * s, 2)], in_sem.at[s])
         c.start()
         fetch.append(c)
+
+    for c in small:
+        c.wait()
 
     for s in range(pairs):
         fetch[s].wait()
@@ -72,12 +85,10 @@
             norms.append(jnp.sum(wide * wide, axis=0, keepdims=True))
         for m in range(nz // 2):
             at = slice(m * LANES, (m + 1) * LANES)
-            for pair, top, count in ((prods, s * LANES, LANES), (norms, pairs * LANES + s, 1)):
+            for pair, ref in ((prods, part), (norms, part_n)):
                 a, b = pair[0][:, at], pair[1][:, at]
-                part[2 * m, top:top + count, :] = jnp.where(low, a, swap(b))
-                part[2 * m + 1, top:top + count, :] = jnp.where(low, swap(a), b)
-    for d in range(nz):
-        part[d, pairs * LANES + pairs:, :] = jnp.zeros((EXTRA - pairs, LANES), F32)
+                ref[2 * m, s] = jnp.where(low, a, swap(b))
+                ref[2 * m + 1, s] = jnp.where(low, swap(a), b)
     gather[me_z] = snaps_ref[me_r]
 
     pl.semaphore_wait(barrier, len(greet))
@@ -154,28 +165,52 @@
     def arm(s, way):
         return hops if (s < (pairs + 1) // 2) == (way == 0) else hops - 1
 
-    def span(s):
-        return slice(s * LANES, (s + 1) * LANES + (EXTRA if s == pairs - 1 else 0))
+    def encode(v, ref):
+        most = jnp.maximum(jnp.max(jnp.abs(v), axis=0, keepdims=True), 1e-30)
+        q = jnp.round(v * (TOP / most)).astype(jnp.int32)
+        mask = (1 << FIELD) - 1
+        q_a, q_b, q_c = q[:LANES - 2 * THIRD], q[LANES - 2 * THIRD:WORDS], q[WORDS:]
+        ref[:THIRD, :] = (q_a[:THIRD] & mask) | (q_c << FIELD)
+        ref[THIRD:LANES - 2 * THIRD, :] = q_a[THIRD:] & mask
+        ref[LANES - 2 * THIRD:, :] = (q_b & mask) | ((q_c >> (32 - FIELD)) << FIELD)
+        return most * (1.0 / TOP)
+
+    def decode(ref, unit):
+        w = ref[...]
+        w_a, w_b = w[:LANES - 2 * THIRD], w[LANES - 2 * THIRD:]
+        q_c = ((w_b >> FIELD) << (32 - FIELD)) | lax.shift_right_logical(w_a[:THIRD], jnp.full((THIRD, LANES), FIELD, jnp.int32))
+        q = jnp.concatenate([(w << (32 - FIELD)) >> (32 - FIELD), q_c], axis=0)
+        return q.astype(F32) * unit
 
     rs = {}
+
+    def arrived(way, t, s):
+        for c in rs[way, t, s]:
+            c.wait_recv()
+        n = recv_n[way, t, s]
+        return decode(recv_w.at[way, t, s], n[:1]), n[1:]
 
     def send(way, t, s):
         sign = 1 if way == 0 else -1
-        sp = span(s)
-        rows = pl.ds(sp.start, sp.stop - sp.start)
         dest = ahead(me_z, sign * (arm(s, way) - t), nz)
+        value, norm = part[dest, s], part_n[dest, s]
         if t == 0:
-            src = part.at[dest, rows]
+            words, norms = first_w.at[way, s], first_n.at[way, s]
         else:
-            rs[way, t - 1, s].wait_recv()
-            recv[way, t - 1, sp, :] = recv[way, t - 1, sp, :] + part[dest, sp, :]
-            src = recv.at[way, t - 1, rows]
-        c = remote(src, recv.at[way, t, rows], rs_s.at[way, t, s], rs_r.at[way, t, s], {"col": ahead(me_z, sign, nz)})
-        c.start()
-        rs[way, t, s] = c
-        pending.append(c)
-
-    order = [pairs - 1] + list(range(pairs - 1))
+            more, more_n = arrived(way, t - 1, s)
+            value, norm = value + more, norm + more_n
+            words, norms = recv_w.at[way, t - 1, s], recv_n.at[way, t - 1, s]
+        norms[:1, :] = encode(value, words)
+        norms[1:, :] = norm
+        to = {"col": ahead(me_z, sign, nz)}
+        rs[way, t, s] = (
+            remote(words, recv_w.at[way, t, s], rs_s.at[way, t, s], rs_r.at[way, t, s], to),
+            remote(norms, recv_n.at[way, t, s], rn_s.at[way, t, s], rn_r.at[way, t, s], to),
+        )
+        for c in rs[way, t, s]:
+            c.start()
+            pending.append(c)
+
     total_steps = hops * pairs
     gap = 2 if total_steps >= 4 * hops else 1
     done = min(gap * hops + 1, total_steps - 1)
@@ -186,7 +221,7 @@
     pass_on(0)
     next_hop = 1
     for t in range(hops):
-        for s in order:
+        for s in range(pairs):
             for way in (0, 1):
                 if t < arm(s, way):
                     send(way, t, s)
@@ -206,18 +241,12 @@
         sweep(0, pivots)
 
     outgoing = {}
-    norms = None
-    for s in order:
-        sp = span(s)
-        total = part[me_z, sp, :]
+    for s in range(pairs):
+        total, norm = part[me_z, s], part_n[me_z, s]
         for way in (0, 1):
-            last = arm(s, way) - 1
-            rs[way, last, s].wait_recv()
-            total = total + recv[way, last, sp, :]
-        if s == pairs - 1:
-            norms = total[LANES:]
-        up, down = total[:HALF], total[HALF:LANES]
-        norm = norms[s:s + 1, :]
+            more, more_n = arrived(way, arm(s, way) - 1, s)
+            total, norm = total + more, norm + more_n
+        up, down = total[:HALF], total[HALF:]
         for f, packed, row in (
             (2 * s, jnp.where(low, up, swap(down)), norm),
             (2 * s + 1, jnp.where(low, swap(up), down), swap(norm)),
@@ -329,22 +358,27 @@
 def solution(mesh):
     nf, nr, nz = mesh.shape["freq"], mesh.shape["row"], mesh.shape["col"]
     pairs, hops = nr // 2, nz // 2
-    rows = pairs * LANES + EXTRA
     dma = pltpu.SemaphoreType.DMA
 
     def body(snapshots, replicas, level_index, loading_iters):
         freqs, sensors, cands = snapshots.shape[0], snapshots.shape[1], replicas.shape[3]
         vmem = pl.BlockSpec(memory_space=pltpu.VMEM)
-        smem = pl.BlockSpec(memory_space=pltpu.SMEM)
         both = pl.pallas_call(
             functools.partial(kernel, nf, nr, nz),
             out_shape=jax.ShapeDtypeStruct((freqs + EXTRA, LANES), F32),
-            in_specs=[smem, smem, vmem, pl.BlockSpec(memory_space=pl.ANY)],
+            in_specs=[pl.BlockSpec(memory_space=pl.ANY)] * 4,
             out_specs=vmem,
             scratch_shapes=[
+                pltpu.SMEM((freqs,), jnp.int32),
+                pltpu.SMEM((freqs,), jnp.int32),
+                pltpu.VMEM((freqs, sensors, LANES), jnp.bfloat16),
                 pltpu.VMEM((freqs, 2 * sensors, cands), jnp.bfloat16),
-                pltpu.VMEM((nz, rows, LANES), F32),
-                pltpu.VMEM((2, hops, rows, LANES), F32),
+                pltpu.VMEM((nz, pairs, LANES, LANES), F32),
+                pltpu.VMEM((nz, pairs, 1, LANES), F32),
+                pltpu.VMEM((2, pairs, WORDS, LANES), jnp.int32),
+                pltpu.VMEM((2, pairs, 2, LANES), F32),
+                pltpu.VMEM((2, hops, pairs, WORDS, LANES), jnp.int32),
+                pltpu.VMEM((2, hops, pairs, 2, LANES), F32),
                 pltpu.VMEM((nz, sensors, LANES), jnp.bfloat16),
                 pltpu.VMEM((HALF, LANES), F32),
                 pltpu.VMEM((HALF, LANES), F32),
@@ -353,7 +387,8 @@
                 pltpu.VMEM((nz, 1, LANES), F32),
                 pltpu.VMEM((nr, 1, LANES), F32),
                 pltpu.VMEM((nf, nr, 1, LANES), F32),
-                dma((pairs,)),
+                dma((pairs + 3,)),
+                dma((2, hops, pairs)), dma((2, hops, pairs)),
                 dma((2, hops, pairs)), dma((2, hops, pairs)),
                 dma((2, hops)), dma((2, hops)),
                 dma((nr,)), dma((nr,)),

time: 91.6 us -> 83.3 us (0.909)
  Pallas kernels: 90.7 us -> 82.5 us
    pallas_call x1, Pallas kernels: 89.4 us -> 81.2 us  [body(): pl.pallas_call(functools.partial(kernel, nf, nr, nz), out_shape=jax.Shape...]
where the time goes in v3:
time: 83.3 us; the launch traced here: 83.1 us
  Pallas kernels  82.5 us (99%)
    pallas_call x1, Pallas kernels, body(): pl.pallas_call(functools.partial(kernel, nf, nr, nz), out_shape=jax.Shape...  81.2 us

profile of v3, /device:TPU:1, one launch (start us, length us, event | category | flops | bytes accessed | tf_op | source)
XLA Modules:
  0.0 83.1 jit_solution(1940556210181521711)
XLA Ops:
  0.6 81.2 %mvdr.1.both_ref = f32[16,128]{1,0:T(8,128)} custom-call(s32[8]{0:T(128)} %lvl_hbm.1, s32[8]{0:T(128)} %it_hbm.1, bf16[8,64,128]{2,1,0:T(8,128)(2,1)} %snaps_hbm.1, bf16[8,128,1024]{2,1,0:T(8,128)(2,1)} %bitcast.2), custom_call_target="tpu_custom_call" | custom-call | tf_op jit(solution)/shard_map/mvdr/pallas_call | solution.py:366
  81.8 1.3 %split.1 = (f32[8,64]{1,0:T(8,128)}, f32[1,64]{1,0:T(1,128)}) custom-call(f32[16,128]{1,0:T(8,128)} %mvdr.1.both_ref), custom_call_target="tpu_custom_call" | custom-call | tf_op jit(solution)/shard_map/split/pallas_call | solution.py:401

commit v4 on v3

--- a/solution.py
+++ b/solution.py
@@ -61,12 +61,12 @@
 
     small = []
     for i, (src, dst) in enumerate(((snaps_hbm, snaps_ref), (lvl_hbm, lvl_ref), (it_hbm, it_ref))):
-        c = pltpu.make_async_copy(src, dst, in_sem.at[pairs + i])
+        c = pltpu.make_async_copy(src, dst, in_sem.at[freqs + i])
         c.start()
         small.append(c)
     fetch = []
-    for s in range(pairs):
-        c = pltpu.make_async_copy(reps_hbm.at[pl.ds(2 * s, 2)], reps.at[pl.ds(2 * s, 2)], in_sem.at[s])
+    for f in range(freqs):
+        c = pltpu.make_async_copy(reps_hbm.at[f], reps.at[f], in_sem.at[f])
         c.start()
         fetch.append(c)
 
@@ -74,9 +74,9 @@
         c.wait()
 
     for s in range(pairs):
-        fetch[s].wait()
         prods, norms = [], []
-        for f in (2 * s, 2 * s + 1):
+        for f in (s, s + pairs):
+            fetch[f].wait()
             snap = snaps_ref[f].astype(F32)
             stacked = jnp.concatenate([snap * sign_hi, swap(snap)], axis=0)
             cols = reps[f]
@@ -212,33 +212,30 @@
             pending.append(c)
 
     total_steps = hops * pairs
-    gap = 2 if total_steps >= 4 * hops else 1
-    done = min(gap * hops + 1, total_steps - 1)
-    sweeps = list(range(done + 1, total_steps - 1))
+    gap = 3 if total_steps > 3 * hops + 4 else 1
+    done = min(gap * (hops - 1) + 4, total_steps - 1)
     pivots = HALF // 2
-    cuts = [pivots * i // len(sweeps) for i in range(len(sweeps) + 1)] if sweeps else []
+    swept, share = 0, 3
     step = 0
     pass_on(0)
     next_hop = 1
     for t in range(hops):
         for s in range(pairs):
+            if next_hop < hops and step >= gap * next_hop:
+                pass_on(next_hop)
+                next_hop += 1
             for way in (0, 1):
                 if t < arm(s, way):
                     send(way, t, s)
-            if step >= gap * next_hop and next_hop < hops:
-                pass_on(next_hop)
-                next_hop += 1
             if step == done:
                 while next_hop < hops:
                     pass_on(next_hop)
                     next_hop += 1
                 gram_done()
-            if step in sweeps:
-                i = sweeps.index(step)
-                sweep(cuts[i], cuts[i + 1])
+            elif step > done:
+                sweep(swept, swept + share)
+                swept += share
             step += 1
-    if not sweeps:
-        sweep(0, pivots)
 
     outgoing = {}
     for s in range(pairs):
@@ -248,8 +245,8 @@
             total, norm = total + more, norm + more_n
         up, down = total[:HALF], total[HALF:]
         for f, packed, row in (
-            (2 * s, jnp.where(low, up, swap(down)), norm),
-            (2 * s + 1, jnp.where(low, swap(up), down), swap(norm)),
+            (s, jnp.where(low, up, swap(down)), norm),
+            (s + pairs, jnp.where(low, swap(up), down), swap(norm)),
         ):
             xsend[f, :HALF, :] = packed
             xsend[f, HALF:, :] = jnp.broadcast_to(row, (EXTRA, LANES))
@@ -264,6 +261,7 @@
             def _(f=f):
                 xrecv[f] = xsend[f]
 
+    sweep(swept, pivots)
     for q in range(nr):
         @pl.when(me_r != q)
         def _(q=q):
@@ -387,7 +385,7 @@
                 pltpu.VMEM((nz, 1, LANES), F32),
                 pltpu.VMEM((nr, 1, LANES), F32),
                 pltpu.VMEM((nf, nr, 1, LANES), F32),
-                dma((pairs + 3,)),
+                dma((freqs + 3,)),
                 dma((2, hops, pairs)), dma((2, hops, pairs)),
                 dma((2, hops, pairs)), dma((2, hops, pairs)),
                 dma((2, hops)), dma((2, hops)),

time: 83.3 us -> 79.8 us (0.958)
  Pallas kernels: 82.5 us -> 79 us
    pallas_call x1, Pallas kernels: 81.2 us -> 77.7 us  [body(): pl.pallas_call(functools.partial(kernel, nf, nr, nz), out_shape=jax.Shape...]
where the time goes in v4:
time: 79.8 us; the launch traced here: 79.6 us
  Pallas kernels  79 us (99%)
    pallas_call x1, Pallas kernels, body(): pl.pallas_call(functools.partial(kernel, nf, nr, nz), out_shape=jax.Shape...  77.7 us

profile of v4, /device:TPU:1, one launch (start us, length us, event | category | flops | bytes accessed | tf_op | source)
XLA Modules:
  0.0 79.6 jit_solution(15668746124061809646)
XLA Ops:
  0.6 77.7 %mvdr.1.both_ref = f32[16,128]{1,0:T(8,128)} custom-call(s32[8]{0:T(128)} %lvl_hbm.1, s32[8]{0:T(128)} %it_hbm.1, bf16[8,64,128]{2,1,0:T(8,128)(2,1)} %snaps_hbm.1, bf16[8,128,1024]{2,1,0:T(8,128)(2,1)} %bitcast.2), custom_call_target="tpu_custom_call" | custom-call | tf_op jit(solution)/shard_map/mvdr/pallas_call | solution.py:364
  78.3 1.3 %split.1 = (f32[8,64]{1,0:T(8,128)}, f32[1,64]{1,0:T(1,128)}) custom-call(f32[16,128]{1,0:T(8,128)} %mvdr.1.both_ref), custom_call_target="tpu_custom_call" | custom-call | tf_op jit(solution)/shard_map/split/pallas_call | solution.py:399

commit v5 on v4

--- a/solution.py
+++ b/solution.py
@@ -13,10 +13,10 @@
 LANES = 128
 HALF = 64
 EXTRA = 8
-WORDS = 88
-THIRD = 40
-FIELD = 21
-TOP = 1048575.0
+WORDS = 80
+GROUP = 16
+FIELD = 20
+TOP = 524287.0
 GAIN_TARGET = 0.5
 MESH_ID = pl.DeviceIdType.MESH
 F32 = jnp.float32
@@ -91,6 +91,46 @@
                 ref[2 * m + 1, s] = jnp.where(low, swap(a), b)
     gather[me_z] = snaps_ref[me_r]
 
+    def arm(s, way):
+        return hops if (s < (pairs + 1) // 2) == (way == 0) else hops - 1
+
+    def encode(v, ref):
+        most = jnp.maximum(jnp.max(jnp.abs(v), axis=0, keepdims=True), 1e-30)
+        q = jnp.round(v * (TOP / most)).astype(jnp.int32) & ((1 << FIELD) - 1)
+        g = [q[i * GROUP:(i + 1) * GROUP] for i in range(8)]
+        g_6, g_7 = g[6], g[7]
+        tops = (
+            g[5],
+            lax.shift_right_logical(g[5], jnp.full((GROUP, LANES), 12, jnp.int32)) | (g_6 << 8),
+            g_6 >> 4,
+            (g_6 >> 16) | (g_7 << 4),
+            g_7 >> 8,
+        )
+        for i, top in enumerate(tops):
+            ref[i * GROUP:(i + 1) * GROUP, :] = g[i] | (top << FIELD)
+        return most * (1.0 / TOP)
+
+    def decode(ref, unit):
+        w = ref[...]
+        t = lax.shift_right_logical(w, jnp.full((WORDS, LANES), FIELD, jnp.int32))
+        t = [t[i * GROUP:(i + 1) * GROUP] for i in range(5)]
+        high = jnp.concatenate([
+            t[0] | (t[1] << 12),
+            (t[1] >> 8) | (t[2] << 4) | (t[3] << 16),
+            (t[3] >> 4) | (t[4] << 8),
+        ], axis=0)
+        q = jnp.concatenate([w, high], axis=0)
+        return ((q << (32 - FIELD)) >> (32 - FIELD)).astype(F32) * unit
+
+    def target(way, t, s):
+        return ahead(me_z, (1 if way == 0 else -1) * (arm(s, way) - t), nz)
+
+    for s in range(pairs):
+        for way in (0, 1):
+            dest = target(way, 0, s)
+            first_n[way, s, :1, :] = encode(part[dest, s], first_w.at[way, s])
+            first_n[way, s, 1:, :] = part_n[dest, s]
+
     pl.semaphore_wait(barrier, len(greet))
     pending = []
 
@@ -143,8 +183,8 @@
             pivots = re0 | re1 | im0 | im1
             tile = mat[...]
             row0, row1 = mat[pl.ds(k, 1), :], mat[pl.ds(k + 1, 1), :]
+            a, br, bi, c = at(row0, re0), at(row0, re1), at(row0, im1), at(row1, re1)
             c0r, c0i, c1r, c1i = at(tile, re0), at(tile, im0), at(tile, re1), at(tile, im1)
-            a, br, bi, c = at(row0, re0), at(row0, re1), at(row0, im1), at(row1, re1)
             r0 = jnp.where(re0, -1.0, jnp.where(pivots, 0.0, row0))
             r1 = jnp.where(re1, -1.0, jnp.where(pivots, 0.0, row1))
             j0, j1 = swap(r0) * sign_lo, swap(r1) * sign_lo
@@ -162,26 +202,6 @@
 
         lax.fori_loop(first, last, one, 0)
 
-    def arm(s, way):
-        return hops if (s < (pairs + 1) // 2) == (way == 0) else hops - 1
-
-    def encode(v, ref):
-        most = jnp.maximum(jnp.max(jnp.abs(v), axis=0, keepdims=True), 1e-30)
-        q = jnp.round(v * (TOP / most)).astype(jnp.int32)
-        mask = (1 << FIELD) - 1
-        q_a, q_b, q_c = q[:LANES - 2 * THIRD], q[LANES - 2 * THIRD:WORDS], q[WORDS:]
-        ref[:THIRD, :] = (q_a[:THIRD] & mask) | (q_c << FIELD)
-        ref[THIRD:LANES - 2 * THIRD, :] = q_a[THIRD:] & mask
-        ref[LANES - 2 * THIRD:, :] = (q_b & mask) | ((q_c >> (32 - FIELD)) << FIELD)
-        return most * (1.0 / TOP)
-
-    def decode(ref, unit):
-        w = ref[...]
-        w_a, w_b = w[:LANES - 2 * THIRD], w[LANES - 2 * THIRD:]
-        q_c = ((w_b >> FIELD) << (32 - FIELD)) | lax.shift_right_logical(w_a[:THIRD], jnp.full((THIRD, LANES), FIELD, jnp.int32))
-        q = jnp.concatenate([(w << (32 - FIELD)) >> (32 - FIELD), q_c], axis=0)
-        return q.astype(F32) * unit
-
     rs = {}
 
     def arrived(way, t, s):
@@ -191,18 +211,15 @@
         return decode(recv_w.at[way, t, s], n[:1]), n[1:]
 
     def send(way, t, s):
-        sign = 1 if way == 0 else -1
-        dest = ahead(me_z, sign * (arm(s, way) - t), nz)
-        value, norm = part[dest, s], part_n[dest, s]
         if t == 0:
             words, norms = first_w.at[way, s], first_n.at[way, s]
         else:
+            dest = target(way, t, s)
             more, more_n = arrived(way, t - 1, s)
-            value, norm = value + more, norm + more_n
             words, norms = recv_w.at[way, t - 1, s], recv_n.at[way, t - 1, s]
-        norms[:1, :] = encode(value, words)
-        norms[1:, :] = norm
-        to = {"col": ahead(me_z, sign, nz)}
+            norms[:1, :] = encode(part[dest, s] + more, words)
+            norms[1:, :] = part_n[dest, s] + more_n
+        to = {"col": ahead(me_z, 1 if way == 0 else -1, nz)}
         rs[way, t, s] = (
             remote(words, recv_w.at[way, t, s], rs_s.at[way, t, s], rs_r.at[way, t, s], to),
             remote(norms, recv_n.at[way, t, s], rn_s.at[way, t, s], rn_r.at[way, t, s], to),
@@ -211,6 +228,7 @@
             c.start()
             pending.append(c)
 
+    half = (pairs + 1) // 2
     total_steps = hops * pairs
     gap = 3 if total_steps > 3 * hops + 4 else 1
     done = min(gap * (hops - 1) + 4, total_steps - 1)
@@ -225,8 +243,9 @@
                 pass_on(next_hop)
                 next_hop += 1
             for way in (0, 1):
-                if t < arm(s, way):
-                    send(way, t, s)
+                turn = (s + way * half) % pairs
+                if t < arm(turn, way):
+                    send(way, t, turn)
             if step == done:
                 while next_hop < hops:
                     pass_on(next_hop)
@@ -238,7 +257,7 @@
             step += 1
 
     outgoing = {}
-    for s in range(pairs):
+    for s in sorted(range(pairs), key=lambda s: s % half):
         total, norm = part[me_z, s], part_n[me_z, s]
         for way in (0, 1):
             more, more_n = arrived(way, arm(s, way) - 1, s)
@@ -294,7 +313,7 @@
 
     gain[me_z] = jnp.broadcast_to(mine, (1, LANES))
     copies = []
-    for o in range(1, nz):
+    for o in sorted(range(1, nz), key=lambda o: abs(o - hops)):
         c = remote(gain.at[me_z], gain.at[me_z], qz_s.at[o], qz_r.at[o], {"col": ahead(me_z, o, nz)})
         c.start()
         copies.append(c)

time: 79.8 us -> 77.6 us (0.972)
  Pallas kernels: 79 us -> 76.8 us
    pallas_call x1, Pallas kernels: 77.7 us -> 75.5 us  [body(): pl.pallas_call(functools.partial(kernel, nf, nr, nz), out_shape=jax.Shape...]
where the time goes in v5:
time: 77.6 us; the launch traced here: 77.4 us
  Pallas kernels  76.8 us (99%)
    pallas_call x1, Pallas kernels, body(): pl.pallas_call(functools.partial(kernel, nf, nr, nz), out_shape=jax.Shape...  75.5 us

profile of v5, /device:TPU:1, one launch (start us, length us, event | category | flops | bytes accessed | tf_op | source)
XLA Modules:
  0.0 77.4 jit_solution(14637825661647863088)
XLA Ops:
  0.6 75.5 %mvdr.1.both_ref = f32[16,128]{1,0:T(8,128)} custom-call(s32[8]{0:T(128)} %lvl_hbm.1, s32[8]{0:T(128)} %it_hbm.1, bf16[8,64,128]{2,1,0:T(8,128)(2,1)} %snaps_hbm.1, bf16[8,128,1024]{2,1,0:T(8,128)(2,1)} %bitcast.2), custom_call_target="tpu_custom_call" | custom-call | tf_op jit(solution)/shard_map/mvdr/pallas_call | solution.py:383
  76.1 1.3 %split.1 = (f32[8,64]{1,0:T(8,128)}, f32[1,64]{1,0:T(1,128)}) custom-call(f32[16,128]{1,0:T(8,128)} %mvdr.1.both_ref), custom_call_target="tpu_custom_call" | custom-call | tf_op jit(solution)/shard_map/split/pallas_call | solution.py:418

commit v6 on v5

--- a/solution.py
+++ b/solution.py
@@ -200,7 +200,10 @@
             mat[pl.ds(k + 1, 1), :] = u1
             return carry
 
-        lax.fori_loop(first, last, one, 0)
+        twos = (last - first) // 2
+        lax.fori_loop(0, twos, lambda i, carry: one(first + 2 * i + 1, one(first + 2 * i, carry)), 0)
+        if (last - first) % 2:
+            one(last - 1, 0)
 
     rs = {}
 
@@ -340,8 +343,8 @@
 
     lrecv[me_f, me_r] = lsend[me_r]
     copies = []
-    for of in range(nf):
-        for o in range(nr):
+    for of in sorted(range(nf), key=lambda o: abs(o - nf // 2)):
+        for o in sorted(range(nr), key=lambda o: abs(o - nr // 2)):
             if of or o:
                 to_f, to_r = ahead(me_f, of, nf), ahead(me_r, o, nr)
                 c = remote(lsend.at[to_r], lrecv.at[me_f, me_r], ll_s.at[of, o], ll_r.at[of, o], {"freq": to_f, "row": to_r})

time: 77.6 us -> 77.5 us (level)
  no operation moved by 1% of the time
where the time goes in v6:
time: 77.5 us; the launch traced here: 77.3 us
  Pallas kernels  76.7 us (99%)
    pallas_call x1, Pallas kernels, body(): pl.pallas_call(functools.partial(kernel, nf, nr, nz), out_shape=jax.Shape...  75.4 us

profile of v6, /device:TPU:1, one launch (start us, length us, event | category | flops | bytes accessed | tf_op | source)
XLA Modules:
  0.0 77.3 jit_solution(17010100778067023368)
XLA Ops:
  0.6 75.4 %mvdr.1.both_ref = f32[16,128]{1,0:T(8,128)} custom-call(s32[8]{0:T(128)} %lvl_hbm.1, s32[8]{0:T(128)} %it_hbm.1, bf16[8,64,128]{2,1,0:T(8,128)(2,1)} %snaps_hbm.1, bf16[8,128,1024]{2,1,0:T(8,128)(2,1)} %bitcast.2), custom_call_target="tpu_custom_call" | custom-call | tf_op jit(solution)/shard_map/mvdr/pallas_call | solution.py:386
  76.0 1.3 %split.1 = (f32[8,64]{1,0:T(8,128)}, f32[1,64]{1,0:T(1,128)}) custom-call(f32[16,128]{1,0:T(8,128)} %mvdr.1.both_ref), custom_call_target="tpu_custom_call" | custom-call | tf_op jit(solution)/shard_map/split/pallas_call | solution.py:421
